TPU v7x, 32 devices: a whole 2x2x4 slice. The times are simulated.
32 devices in a mesh: gx: 2 (over x), gy: 4 (over z), gz: 4 (over y, core).
Axes of the slice: x: 2, y: 2, z: 4, core: 2. Of those that a mesh axis runs over, the one named last changes fastest.
Arguments:
- right_side: float32 [128, 256, 1024], P('gx', 'gy', 'gz'), may hold values from -5 to 7
- initial_guess: float32 [128, 256, 1024], P('gx', 'gy', 'gz'), may hold values from -5 to 7
Outputs:
- solution: float32 [128, 256, 1024], P('gx', 'gy', 'gz')
All inputs are finite; a program needn't handle non-finite values.
Results may differ from a plain program's by a relative error of at most 0.000028.
Values sent between devices are 32-bit elements; how exact they have to be, the bound alone decides.
A program may use at most 128 MiB of HBM per device.

v0:
```python
import jax
import jax.numpy as jnp
from jax import lax
from jax.sharding import PartitionSpec as P

COARSE_SWEEPS = 6


relax_weight = 0.8


def passed_along(shard, axis, by):
    devices = lax.axis_size(axis)
    return lax.ppermute(shard, axis, [(i, (i + by) % devices) for i in range(devices)])


def padded_2(block, sides, width):
    for axis, dim in sides:
        count = lax.axis_size(axis)
        forward = [(i, i + 1) for i in range(count - 1)]
        forward.append((count - 1, 0))
        backward = [(target, source) for source, target in forward]
        low = lax.ppermute(
            lax.slice_in_dim(block, block.shape[dim] - width, None, axis=dim), axis, forward
        )
        high = lax.ppermute(lax.slice_in_dim(block, 0, width, axis=dim), axis, backward)
        block = jnp.concatenate([low, block, high], axis=dim)
    return block


def stencil_parts(padded):
    centre = padded[1:-1, 1:-1, 1:-1]
    beside = padded[2:, 1:-1, 1:-1] + padded[:-2, 1:-1, 1:-1]
    beside = beside + padded[1:-1, 2:, 1:-1] + padded[1:-1, :-2, 1:-1]
    beside = beside + padded[1:-1, 1:-1, 2:] + padded[1:-1, 1:-1, :-2]
    return (centre, beside)


def relax_step(centre, beside, source, level_scale):
    return centre + relax_weight * (source / (6.0 * level_scale) - centre + beside / 6.0)


def defect_of(centre, beside, source, level_scale):
    return source - level_scale * (6.0 * centre - beside)


def restrict_along(extended, along):
    inner_count = extended.shape[along] - 1
    lower_side = lax.slice_in_dim(extended, 0, inner_count, 2, along)
    on_points = lax.slice_in_dim(extended, 1, inner_count + 1, 2, along)
    upper_side = lax.slice_in_dim(extended, 2, inner_count + 1, 2, along)
    return 0.25 * lower_side + 0.5 * on_points + 0.25 * upper_side


def restrict_lower(values):
    rim = passed_along(values[-1:], "gx", 1)
    values = restrict_along(jnp.concatenate([rim, values], 0), 0)
    rim = passed_along(values[:, -1:], "gy", 1)
    values = restrict_along(jnp.concatenate([rim, values], 1), 1)
    rim = passed_along(values[:, :, -1:], "gz", 1)
    return restrict_along(jnp.concatenate([rim, values], 2), 2)


def prolong_along(values, rim, along):
    upper_side = jnp.concatenate(
        [lax.slice_in_dim(values, 1, values.shape[along], 1, along), rim], along
    )
    between = 0.5 * (values + upper_side)
    stacked = jnp.stack([values, between], along + 1)
    new_shape = list(values.shape)
    new_shape[along] = 2 * new_shape[along]
    return stacked.reshape(new_shape)


def prolong_upper(values):
    rim = passed_along(values[:1], "gx", -1)
    values = prolong_along(values, rim, 0)
    rim = passed_along(values[:, :1], "gy", -1)
    values = prolong_along(values, rim, 1)
    rim = passed_along(values[:, :, :1], "gz", -1)
    return prolong_along(values, rim, 2)


def near_faces(values):
    return padded_2(values, (("gx", 0), ("gy", 1), ("gz", 2)), 1)


def single_sweep(approx, source, level_scale):
    centre, beside = stencil_parts(near_faces(approx))
    return relax_step(centre, beside, source, level_scale)


def paired_sweeps(approx, source, level_scale):
    approx = single_sweep(approx, source, level_scale)
    return single_sweep(approx, source, level_scale)


def coarse_relax(padded, approx, source):
    beside = padded[2:, 1:-1] + padded[:-2, 1:-1]
    beside = beside + padded[1:-1, 2:] + padded[1:-1, :-2]
    beside = beside + jnp.roll(approx, -1, 2) + jnp.roll(approx, 1, 2)
    return relax_step(approx, beside, source, 0.0625)


def coarsest_solve(source):
    thickness = source.shape[2]
    whole_source = lax.all_gather(source, "gz", axis=2, tiled=True)
    margin = COARSE_SWEEPS - 1
    padded_source = padded_2(whole_source, (("gx", 0), ("gy", 1)), margin)
    empty = jnp.zeros_like(padded_source)
    approx = relax_step(empty, empty, padded_source, 0.0625)
    size_first = padded_source.shape[0]
    size_second = padded_source.shape[1]
    for sweep_index in range(margin):
        inner = sweep_index + 1
        inner_source = padded_source[inner : size_first - inner, inner : size_second - inner]
        approx = coarse_relax(approx, approx[1:-1, 1:-1], inner_source)
    return lax.dynamic_slice_in_dim(approx, lax.axis_index("gz") * thickness, thickness, 2)


def multigrid_cycle(approx, source, grid_level):
    if grid_level == 2:
        return coarsest_solve(source)
    level_scale = 0.25**grid_level
    approx = paired_sweeps(approx, source, level_scale)
    centre, beside = stencil_parts(near_faces(approx))
    defect_field = defect_of(centre, beside, source, level_scale)
    coarse_source = restrict_lower(defect_field)
    correction = multigrid_cycle(jnp.zeros_like(coarse_source), coarse_source, grid_level + 1)
    approx = approx + prolong_upper(correction)
    return paired_sweeps(approx, source, level_scale)


def shards(right_side, initial_guess):
    cell_count = right_side.size * lax.axis_size("gx") * lax.axis_size("gy") * lax.axis_size("gz")
    totals = lax.psum((jnp.sum(right_side), jnp.sum(initial_guess)), ("gx", "gy", "gz"))
    source = right_side - totals[0] / cell_count
    approx = initial_guess - totals[1] / cell_count
    return multigrid_cycle(approx, source, 0)


def solution(mesh):
    placed = (P("gx", "gy", "gz"), P("gx", "gy", "gz"))
    return jax.shard_map(
        shards, mesh=mesh, in_specs=placed, out_specs=P("gx", "gy", "gz"), check_vma=False
    )
```

profile of v0, /device:TPU:0, one launch (start us, length us, event | category | flops | bytes accessed | tf_op | source)
XLA Modules:
  0.0 586.5 jit_solution(739219115648731776)
XLA Ops:
  0.0 3.9 reduce_sum.19
  3.9 3.9 reduce_sum.18
  7.8 42.2 %all-reduce.2 = (f32[]{:T(128)}, f32[]{:T(128)}) all-reduce(f32[]{:T(128)} %reduce_sum.18, f32[]{:T(128)} %reduce_sum.19), channel_id=1, replica_groups=mesh['gx'=2,'gy'=4,'gz'=4] {'gx','gy','gz'}, use_global_device_ids=true, to_apply=%region_1.0 | all-reduce | flops 2 | bytes 16 | tf_op jit(solution)/shard_map/psum | solution.py:136
  50.7 2.5 broadcast_subtract_fusion
  69.6 2.5 copy.25
  78.7 23.1 %fusion.38 = f32[64,64,256]{2,1,0:T(8,128)S(1)} fusion(f32[64,64,256]{2,1,0:T(8,128)} %copy-done.4, f32[66,66,1]{2,1,0:T(8,128)} %copy.28, f32[66,1,256]{2,1,0:T(1,128)S(1)} %collective-permute-done.2, f32[66,1,256]{2,1,0:T(1,128)S(1)} %collective-permute-done.3, f32[1,64,256]{2,1,0:T(8,128)S(1)} %collective-permute-done, ...), kind=kLoop, calls=%fused_computation.117 | loop fusion | flops 31457280 | bytes 12884004 | tf_op jit(solution)/shard_map/add | solution.py:40
  103.9 2.4 collective-permute-done.7
  108.0 3.0 collective-permute-start.8
  116.4 2.5 copy.29
  119.8 10.8 %collective-permute-start.11 = (f32[66,66,1]{1,2,0:T(1,128)S(1)}, f32[66,66,1]{1,2,0:T(1,128)S(1)}, u32[]{:S(2)}, u32[]{:S(2)}) collective-permute-start(f32[66,66,1]{1,2,0:T(1,128)S(1)} %copy.31), channel_id=1, source_target_pairs={{0,1},{1,2},{2,3},{3,0},{4,5},{5,6},{6,7},{7,4},{8,9},{9,10},{10,1... | collective-permute-start | bytes 52280 | tf_op jit(solution)/shard_map/ppermute | solution.py:23
  135.7 23.1 %fusion.29 = f32[64,64,256]{2,1,0:T(8,128)S(1)} fusion(f32[64,64,256]{2,1,0:T(8,128)} %copy-done.2, f32[66,66,1]{2,1,0:T(8,128)} %copy.32, f32[66,1,256]{2,1,0:T(1,128)S(1)} %collective-permute-done.8, f32[66,1,256]{2,1,0:T(1,128)S(1)} %collective-permute-done.9, f32[1,64,256]{2,1,0:T(8,128)S(1)} %collective-permute-done.6, ...), kind=kLoop, calls=%fused_computation.90 | loop fusion | flops 31457280 | bytes 12884004 | tf_op jit(solution)/shard_map/add | solution.py:40
  165.7 2.7 collective-permute-start.14
  173.8 2.5 copy.33
  180.3 2.6 collective-permute-start.23
  186.2 23.1 %fusion.20 = f32[64,64,256]{2,1,0:T(8,128)S(1)} fusion(f32[66,66,1]{2,1,0:T(8,128)} %copy.36, f32[66,1,256]{2,1,0:T(1,128)S(1)} %collective-permute-done.14, f32[66,1,256]{2,1,0:T(1,128)S(1)} %collective-permute-done.15, f32[1,64,256]{2,1,0:T(8,128)S(1)} %collective-permute-done.12, f32[64,64,256]{2,1,0:T(8,128)} %copy-done, ...), kind=kLoop, calls=%fused_computation.63 | loop fusion | flops 28311552 | bytes 12884004 | tf_op jit(solution)/shard_map/sub | solution.py:44
  210.3 3.3 collective-permute-done.18
  221.0 2.8 slice.764
  223.8 2.8 slice.763
  228.2 4.1 slice.762
  236.5 19.5 %slice.768 = f32[32,32,128]{2,1,0:T(8,128)S(1)} slice(f32[32,32,256]{2,1,0:T(8,128)S(1)} %multiply_add_fusion.1), slice={[0:32:1], [0:32:1], [1:256:2]} | slice | bytes 1048576 | tf_op jit(solution)/shard_map/slice | solution.py:51
  256.0 20.0 %slice.767 = f32[32,32,128]{2,1,0:T(8,128)} slice(f32[32,32,256]{2,1,0:T(8,128)S(1)} %multiply_add_fusion.1), slice={[0:32:1], [0:32:1], [0:256:2]} | slice | bytes 1048576 | tf_op jit(solution)/shard_map/slice | solution.py:50
  276.0 2.6 pad_maximum_fusion.99
  278.7 20.2 %slice.766 = f32[32,32,128]{2,1,0:T(8,128)S(1)} slice(f32[32,32,257]{2,1,0:T(8,128)} %pad_maximum_fusion.99), slice={[0:32:1], [0:32:1], [0:256:2]} | slice | bytes 1048576 | tf_op jit(solution)/shard_map/slice | solution.py:49
  323.0 2.7 collective-permute-start.35
  333.6 2.6 collective-permute-done.39
  338.0 4.1 collective-permute-done.40
  350.7 16.6 %all_gather.3 = f32[16,16,256]{1,0,2:T(8,128)S(1)} all-gather(f32[16,16,64]{1,0,2:T(8,128)} %copy.49), channel_id=1, replica_groups=mesh['gx'=2,'gy'=4,'gz'=4] {'gz'}, dimensions={2}, use_global_device_ids=true | all-gather | bytes 327680 | tf_op jit(solution)/shard_map/all_gather | solution.py:107
  370.4 3.3 collective-permute-done.42
  375.0 3.8 collective-permute-start.45
  378.8 6.1 %collective-permute-done.44 = f32[26,5,256]{2,1,0:T(8,128)S(1)} collective-permute-done((f32[26,5,256]{2,1,0:T(8,128)S(1)}, f32[26,5,256]{2,1,0:T(8,128)S(1)}, u32[]{:S(2)}, u32[]{:S(2)}) %collective-permute-start.44) | collective-permute-done | bytes 133152 | tf_op jit(solution)/shard_map/ppermute | solution.py:23
  391.0 3.0 collective-permute-done.46
  398.7 6.5 %collective-permute-done.48 = f32[32,32,1]{2,0,1:T(8,128)S(1)} collective-permute-done((f32[32,32,1]{2,0,1:T(8,128)S(1)}, f32[32,32,1]{2,0,1:T(8,128)S(1)}, u32[]{:S(2)}, u32[]{:S(2)}) %collective-permute-start.48) | collective-permute-done | bytes 4128 | tf_op jit(solution)/shard_map/ppermute | solution.py:14
  407.4 3.0 copy.59
  419.2 2.8 collective-permute-start.51
  435.4 2.8 collective-permute-start.57
  445.9 3.1 collective-permute-done.61
  449.4 3.9 collective-permute-start.62
  460.1 2.9 copy.75
  463.0 2.8 fusion.43
  468.2 9.3 %copy.76 = f32[64,64,128,2]{1,0,3,2:T(8,128)} copy(f32[64,64,128,2]{2,0,1,3:T(8,128)} %pad_maximum_fusion.96) | data formatting | bytes 8388608 | tf_op jit(solution)/shard_map/stack | solution.py:69
  477.4 7.7 %copy.77 = f32[64,64,256]{2,1,0:T(8,128)} copy(f32[64,64,256]{1,0,2:T(8,128)} %bitcast.41) | data formatting | bytes 8388608 | tf_op jit(solution)/shard_map/reshape | solution.py:72
  485.2 4.3 add.505
  491.6 2.9 collective-permute-done.65
  496.1 4.2 collective-permute-start.66
  505.7 2.5 copy.78
  515.0 23.1 %fusion.13 = f32[64,64,256]{2,1,0:T(8,128)S(1)} fusion(f32[64,64,256]{2,1,0:T(8,128)} %copy-done.3, f32[66,66,1]{2,1,0:T(8,128)} %copy.81, f32[66,1,256]{2,1,0:T(1,128)S(1)} %collective-permute-done.66, f32[66,1,256]{2,1,0:T(1,128)S(1)} %collective-permute-done.67, f32[1,64,256]{2,1,0:T(8,128)S(1)} %collective-permute-done.64, ...), kind=kLoop, calls=%fused_computation.38 | loop fusion | flops 31457280 | bytes 12884004 | tf_op jit(solution)/shard_map/add | solution.py:40
  553.2 2.5 copy.82
  562.3 24.1 %fusion.4 = f32[64,64,256]{2,1,0:T(8,128)} fusion(f32[64,64,256]{2,1,0:T(8,128)} %copy-done.1, f32[66,66,1]{2,1,0:T(8,128)} %copy.85, f32[66,1,256]{2,1,0:T(1,128)S(1)} %collective-permute-done.72, f32[66,1,256]{2,1,0:T(1,128)S(1)} %collective-permute-done.73, f32[1,64,256]{2,1,0:T(8,128)S(1)} %collective-permute-done.70, ...), kind=kLoop, calls=%fused_computation.11 | loop fusion | flops 31457280 | bytes 12884004 | tf_op jit(solution)/shard_map/add | solution.py:40
  (296 shorter events, 207.2 us)
Async XLA Ops:
  53.2 4.6 collective-permute-start.1
  55.6 4.3 collective-permute-start
  59.9 6.2 %collective-permute-start.3 = (f32[66,1,256]{2,1,0:T(1,128)S(1)}, f32[66,1,256]{2,1,0:T(1,128)S(1)}, u32[]{:S(2)}, u32[]{:S(2)}) collective-permute-start(f32[66,1,256]{2,1,0:T(1,128)S(1)} %get-tuple-element.27), channel_id=1, source_target_pairs={{0,4},{4,8},{8,12},{12,0},{1,5},{5,9},{9,13},{13,1},{2,6},{6,10},{... | collective-permute-start | bytes 202760 | tf_op jit(solution)/shard_map/ppermute | solution.py:23
  61.5 5.0 collective-permute-start.2
  101.8 4.5 collective-permute-start.7
  102.5 4.5 collective-permute-start.6
  107.1 6.2 %collective-permute-start.9 = (f32[66,1,256]{2,1,0:T(1,128)S(1)}, f32[66,1,256]{2,1,0:T(1,128)S(1)}, u32[]{:S(2)}, u32[]{:S(2)}) collective-permute-start(f32[66,1,256]{2,1,0:T(1,128)S(1)} %get-tuple-element.25), channel_id=1, source_target_pairs={{0,4},{4,8},{8,12},{12,0},{1,5},{5,9},{9,13},{13,1},{2,6},{6,10},{... | collective-permute-start | bytes 202760 | tf_op jit(solution)/shard_map/ppermute | solution.py:23
  108.0 5.3 collective-permute-start.8
  118.9 11.7 %collective-permute-start.10 = (f32[66,66,1]{1,2,0:T(1,128)S(1)}, f32[66,66,1]{1,2,0:T(1,128)S(1)}, u32[]{:S(2)}, u32[]{:S(2)}) collective-permute-start(f32[66,66,1]{1,2,0:T(1,128)S(1)} %copy.29), channel_id=1, source_target_pairs={{1,0},{2,1},{3,2},{0,3},{5,4},{6,5},{7,6},{4,7},{9,8},{10,9},{11,1... | collective-permute-start | bytes 52280 | tf_op jit(solution)/shard_map/ppermute | solution.py:26
  119.8 13.6 %collective-permute-start.11 = (f32[66,66,1]{1,2,0:T(1,128)S(1)}, f32[66,66,1]{1,2,0:T(1,128)S(1)}, u32[]{:S(2)}, u32[]{:S(2)}) collective-permute-start(f32[66,66,1]{1,2,0:T(1,128)S(1)} %copy.31), channel_id=1, source_target_pairs={{0,1},{1,2},{2,3},{3,0},{4,5},{5,6},{6,7},{7,4},{8,9},{9,10},{10,1... | collective-permute-start | bytes 52280 | tf_op jit(solution)/shard_map/ppermute | solution.py:23
  158.8 4.3 collective-permute-start.13
  160.1 4.3 collective-permute-start.12
  164.5 6.2 %collective-permute-start.15 = (f32[66,1,256]{2,1,0:T(1,128)S(1)}, f32[66,1,256]{2,1,0:T(1,128)S(1)}, u32[]{:S(2)}, u32[]{:S(2)}) collective-permute-start(f32[66,1,256]{2,1,0:T(1,128)S(1)} %get-tuple-element.23), channel_id=1, source_target_pairs={{0,4},{4,8},{8,12},{12,0},{1,5},{5,9},{9,13},{13,1},{2,6},{6,10},{... | collective-permute-start | bytes 202760 | tf_op jit(solution)/shard_map/ppermute | solution.py:23
  165.7 5.0 collective-permute-start.14
  168.4 10.6 %collective-permute-start.22 = (f32[1,32,128]{2,1,0:T(8,128)S(1)}, f32[1,32,128]{2,1,0:T(8,128)S(1)}, u32[]{:S(2)}, u32[]{:S(2)}) collective-permute-start(f32[1,32,128]{2,1,0:T(8,128)S(1)} %broadcast.108), channel_id=1, source_target_pairs={{0,16},{16,0},{1,17},{17,1},{2,18},{18,2},{3,19},{19,3},{4,20},{20... | collective-permute-start | bytes 49160 | tf_op jit(solution)/shard_map/ppermute | solution.py:23
  169.1 9.8 %collective-permute-start.21 = (f32[1,32,128]{2,1,0:T(8,128)S(1)}, f32[1,32,128]{2,1,0:T(8,128)S(1)}, u32[]{:S(2)}, u32[]{:S(2)}) collective-permute-start(f32[1,32,128]{2,1,0:T(8,128)S(1)} %broadcast.108), channel_id=1, source_target_pairs={{16,0},{0,16},{17,1},{1,17},{18,2},{2,18},{19,3},{3,19},{20,4},{4,... | collective-permute-start | bytes 49160 | tf_op jit(solution)/shard_map/ppermute | solution.py:26
  177.2 6.7 %collective-permute-start.17 = (f32[66,66,1]{1,2,0:T(1,128)S(1)}, f32[66,66,1]{1,2,0:T(1,128)S(1)}, u32[]{:S(2)}, u32[]{:S(2)}) collective-permute-start(f32[66,66,1]{1,2,0:T(1,128)S(1)} %copy.35), channel_id=1, source_target_pairs={{0,1},{1,2},{2,3},{3,0},{4,5},{5,6},{6,7},{7,4},{8,9},{9,10},{10,1... | collective-permute-start | bytes 52280 | tf_op jit(solution)/shard_map/ppermute | solution.py:23
  177.2 5.7 collective-permute-start.16
  179.1 31.2 %collective-permute-start.24 = (f32[34,1,128]{2,1,0:T(1,128)S(1)}, f32[34,1,128]{2,1,0:T(1,128)S(1)}, u32[]{:S(2)}, u32[]{:S(2)}) collective-permute-start(f32[34,1,128]{2,1,0:T(1,128)S(1)} %get-tuple-element.67), channel_id=1, source_target_pairs={{0,4},{4,8},{8,12},{12,0},{1,5},{5,9},{9,13},{13,1},{2,6},{6,10},{... | collective-permute-start | bytes 52232 | tf_op jit(solution)/shard_map/ppermute | solution.py:23
  180.3 29.9 %collective-permute-start.23 = (f32[34,1,128]{2,1,0:T(1,128)S(1)}, f32[34,1,128]{2,1,0:T(1,128)S(1)}, u32[]{:S(2)}, u32[]{:S(2)}) collective-permute-start(f32[34,1,128]{2,1,0:T(1,128)S(1)} %get-tuple-element.68), channel_id=1, source_target_pairs={{4,0},{8,4},{12,8},{0,12},{5,1},{9,5},{13,9},{1,13},{6,2},{10,6},{... | collective-permute-start | bytes 52232 | tf_op jit(solution)/shard_map/ppermute | solution.py:26
  209.3 4.3 collective-permute-start.18
  215.0 11.6 %collective-permute-start.19 = (f32[32,1,256]{2,1,0:T(1,128)S(1)}, f32[32,1,256]{2,1,0:T(1,128)S(1)}, u32[]{:S(2)}, u32[]{:S(2)}) collective-permute-start(f32[32,1,256]{2,1,0:T(1,128)S(1)} %slice.941), channel_id=1, source_target_pairs={{0,4},{4,8},{8,12},{12,0},{1,5},{5,9},{9,13},{13,1},{2,6},{6,10},{... | collective-permute-start | bytes 98312 | tf_op jit(solution)/shard_map/ppermute | solution.py:14
  219.2 16.1 %collective-permute-start.26 = (f32[34,34,1]{1,2,0:T(1,128)S(1)}, f32[34,34,1]{1,2,0:T(1,128)S(1)}, u32[]{:S(2)}, u32[]{:S(2)}) collective-permute-start(f32[34,34,1]{1,2,0:T(1,128)S(1)} %copy.39), channel_id=1, source_target_pairs={{0,1},{1,2},{2,3},{3,0},{4,5},{5,6},{6,7},{7,4},{8,9},{9,10},{10,1... | collective-permute-start | bytes 13880 | tf_op jit(solution)/shard_map/ppermute | solution.py:23
  219.2 15.6 %collective-permute-start.25 = (f32[34,34,1]{1,2,0:T(1,128)S(1)}, f32[34,34,1]{1,2,0:T(1,128)S(1)}, u32[]{:S(2)}, u32[]{:S(2)}) collective-permute-start(f32[34,34,1]{1,2,0:T(1,128)S(1)} %copy.37), channel_id=1, source_target_pairs={{1,0},{2,1},{3,2},{0,3},{5,4},{6,5},{7,6},{4,7},{9,8},{10,9},{11,1... | collective-permute-start | bytes 13880 | tf_op jit(solution)/shard_map/ppermute | solution.py:26
  234.4 41.6 %collective-permute-start.20 = (f32[32,32,1]{2,1,0:T(8,128)S(1)}, f32[32,32,1]{2,1,0:T(8,128)}, u32[]{:S(2)}, u32[]{:S(2)}) collective-permute-start(f32[32,32,1]{2,1,0:T(8,128)S(1)} %slice.942), channel_id=1, source_target_pairs={{0,1},{1,2},{2,3},{3,0},{4,5},{5,6},{6,7},{7,4},{8,9},{9,10},{10,1... | collective-permute-start | bytes 12296 | tf_op jit(solution)/shard_map/ppermute | solution.py:14
  305.5 5.7 collective-permute-start.30
  321.5 5.7 collective-permute-start.36
  323.0 4.2 collective-permute-start.35
  336.3 5.7 collective-permute-start.40
  342.4 4.8 collective-permute-start.41
  368.3 5.4 collective-permute-start.42
  369.0 5.8 collective-permute-start.43
  374.9 10.0 %collective-permute-start.44 = (f32[26,5,256]{2,1,0:T(8,128)S(1)}, f32[26,5,256]{2,1,0:T(8,128)S(1)}, u32[]{:S(2)}, u32[]{:S(2)}) collective-permute-start(f32[26,5,256]{2,1,0:T(8,128)S(1)} %get-tuple-element.91), channel_id=1, source_target_pairs={{0,4},{4,8},{8,12},{12,0},{1,5},{5,9},{9,13},{13,1},{2,6},{6,10},{... | collective-permute-start | bytes 399368 | tf_op jit(solution)/shard_map/ppermute | solution.py:23
  375.0 11.3 %collective-permute-start.45 = (f32[26,5,256]{2,1,0:T(8,128)S(1)}, f32[26,5,256]{2,1,0:T(8,128)S(1)}, u32[]{:S(2)}, u32[]{:S(2)}) collective-permute-start(f32[26,5,256]{2,1,0:T(8,128)S(1)} %get-tuple-element.92), channel_id=1, source_target_pairs={{4,0},{8,4},{12,8},{0,12},{5,1},{9,5},{13,9},{1,13},{6,2},{10,6},{... | collective-permute-start | bytes 399368 | tf_op jit(solution)/shard_map/ppermute | solution.py:26
  398.2 7.0 %collective-permute-start.48 = (f32[32,32,1]{2,0,1:T(8,128)S(1)}, f32[32,32,1]{2,0,1:T(8,128)S(1)}, u32[]{:S(2)}, u32[]{:S(2)}) collective-permute-start(f32[32,32,1]{2,0,1:T(8,128)S(1)} %bitcast.47), channel_id=1, source_target_pairs={{0,3},{1,0},{2,1},{3,2},{4,7},{5,4},{6,5},{7,6},{8,11},{9,8},{10,9... | collective-permute-start | bytes 12296 | tf_op jit(solution)/shard_map/ppermute | solution.py:14
  418.1 5.7 collective-permute-start.52
  419.2 4.6 collective-permute-start.51
  434.3 5.6 collective-permute-start.58
  435.4 4.5 collective-permute-start.57
  449.4 5.5 collective-permute-start.62
  489.5 5.0 collective-permute-start.65
  490.1 5.8 collective-permute-start.64
  496.0 6.6 %collective-permute-start.67 = (f32[66,1,256]{2,1,0:T(1,128)S(1)}, f32[66,1,256]{2,1,0:T(1,128)S(1)}, u32[]{:S(2)}, u32[]{:S(2)}) collective-permute-start(f32[66,1,256]{2,1,0:T(1,128)S(1)} %get-tuple-element.21), channel_id=1, source_target_pairs={{0,4},{4,8},{8,12},{12,0},{1,5},{5,9},{9,13},{13,1},{2,6},{6,10},{... | collective-permute-start | bytes 202760 | tf_op jit(solution)/shard_map/ppermute | solution.py:23
  496.1 6.6 %collective-permute-start.66 = (f32[66,1,256]{2,1,0:T(1,128)S(1)}, f32[66,1,256]{2,1,0:T(1,128)S(1)}, u32[]{:S(2)}, u32[]{:S(2)}) collective-permute-start(f32[66,1,256]{2,1,0:T(1,128)S(1)} %get-tuple-element.22), channel_id=1, source_target_pairs={{4,0},{8,4},{12,8},{0,12},{5,1},{9,5},{13,9},{1,13},{6,2},{10,6},{... | collective-permute-start | bytes 202760 | tf_op jit(solution)/shard_map/ppermute | solution.py:26
  538.1 4.3 collective-permute-start.71
  538.7 4.4 collective-permute-start.70
  543.2 6.2 %collective-permute-start.73 = (f32[66,1,256]{2,1,0:T(1,128)S(1)}, f32[66,1,256]{2,1,0:T(1,128)S(1)}, u32[]{:S(2)}, u32[]{:S(2)}) collective-permute-start(f32[66,1,256]{2,1,0:T(1,128)S(1)} %get-tuple-element.19), channel_id=1, source_target_pairs={{0,4},{4,8},{8,12},{12,0},{1,5},{5,9},{9,13},{13,1},{2,6},{6,10},{... | collective-permute-start | bytes 202760 | tf_op jit(solution)/shard_map/ppermute | solution.py:23
  545.6 4.5 collective-permute-start.72
  (33 other events, 151.9 us)
where the time goes:
time: 596 us; the launch traced here: 587 us
  local copies, waits for them, and re-layouts  168 us (28%)
  other arithmetic  160 us (27%)
  waiting for transfers between devices  100 us (17%)
  starting transfers between devices  97.3 us (16%)
  blocking collectives  58.8 us (10%)
    add x12, other arithmetic, relax_step(): centre + relax_weight * (source / (6.0 * level_scale) - centre + beside /...  97.4 us
    ppermute x32, waiting for transfers between devices, padded_2(): lax.ppermute(lax.slice_in_dim(block, block.shape[dim] - width, None, axis...  58.3 us
    ppermute x32, starting transfers between devices, padded_2(): lax.ppermute(lax.slice_in_dim(block, 0, width, axis=dim), axis, backward)  46.2 us
    psum x1, blocking collectives, shards(): lax.psum((jnp.sum(right_side), jnp.sum(initial_guess)), ('gx', 'gy', 'gz'))  42.2 us
    ppermute x32, starting transfers between devices, padded_2(): lax.ppermute(lax.slice_in_dim(block, block.shape[dim] - width, None, axis...  39 us
    slice x20, local copies, waits for them, and re-layouts, padded_2(): lax.slice_in_dim(block, 0, width, axis=dim)  28.5 us
    slice x4, local copies, waits for them, and re-layouts, restrict_along(): lower_side = lax.slice_in_dim(extended, 0, inner_count, 2, along)  26.7 us
    ppermute x12, waiting for transfers between devices, passed_along(): lax.ppermute(shard, axis, [(i, (i + by) % devices) for i in range(devices)])  25.9 us
  transfers between devices with their start and end apart: 76, of which 56 were waited for; matrix products, arithmetic and copies ran while one was open for 19% of the time, Pallas kernels for 0%

commit v1 on v0

v1 whole, which is shorter than its diff:
```python
import functools
import itertools

import jax
import jax.numpy as jnp
from jax import lax
from jax.experimental import pallas as pl
from jax.experimental.pallas import tpu as pltpu
from jax.sharding import PartitionSpec as P

COARSE_SWEEPS = 6
LANES = 128
AXES = ("gx", "gy", "gz")
relax_weight = 0.8


def dot_exact(a, w):
    hi = a.astype(jnp.bfloat16)
    rest = a - hi.astype(jnp.float32)
    mid = rest.astype(jnp.bfloat16)
    low = (rest - mid.astype(jnp.float32)).astype(jnp.bfloat16)
    dot = functools.partial(jnp.dot, preferred_element_type=jnp.float32)
    return dot(hi, w) + (dot(mid, w) + dot(low, w))


def iotas(shape):
    return (
        lax.broadcasted_iota(jnp.int32, shape, 0),
        lax.broadcasted_iota(jnp.int32, shape, 1),
    )


def restrict_matrix(rows, cols, count, wrap=None):
    r, c = iotas((rows, cols))
    w = jnp.where(r == 2 * c, 0.5, 0.0) + jnp.where(jnp.abs(r - 2 * c) == 1, 0.25, 0.0)
    w = jnp.where((c < count) & (r < 2 * count), w, 0.0)
    if wrap is not None:
        w = w + jnp.where((r == wrap) & (c == 0), 0.25, 0.0)
    return w.astype(jnp.bfloat16)


def prolong_matrix(rows, cols, count):
    r, c = iotas((rows, cols))
    w = jnp.where(c == 2 * r, 1.0, 0.0)
    w = w + jnp.where((c == 2 * r + 1) | (c == 2 * r - 1), 0.5, 0.0)
    return jnp.where(r < count, w, 0.0).astype(jnp.bfloat16)


def lane_pad(z):
    return max(z, LANES)


def turn(by):
    return by % LANES if isinstance(by, int) else lax.rem(by, LANES)


def tile_up(h, width):
    return jnp.concatenate([h] * (width // LANES), 1) if width > LANES else h


def buffers(dims):
    f32 = jnp.float32
    out = {}
    rounds = (5, 4, COARSE_SWEEPS - 1)
    for l, (x, y, z) in enumerate(dims):
        zl = lane_pad(z)
        for name in "AB":
            out[f"{name}{l}"] = (x, y, zl)
        if l:
            out[f"G{l}"] = (x, y, zl)
        out[f"yp{l}"] = (2, x, zl)
        out[f"zp{l}"] = (2, y, LANES)
        out[f"hx{l}"] = (rounds[l], 2, y, zl)
        out[f"hy{l}"] = (rounds[l], 2, x, zl)
        out[f"hz{l}"] = (rounds[l], 2, y, LANES)
        for kind in (["r"] if l < 2 else []) + (["p"] if l else []):
            out[f"{kind}x{l}"] = (y, zl)
            out[f"{kind}y{l}"] = (x + 8, zl)
            out[f"{kind}z{l}"] = (y + 8, LANES)
            out[f"{kind}w{l}"] = (y + 8, LANES)
        if l < 2:
            out[f"T{l}"] = (x // 2, y // 2, zl)
            out[f"S{l}"] = (zl // LANES, y, LANES)
            out[f"TH{l}"] = (y // 2, zl)
            out[f"TY{l}"] = (x // 2 + 8, zl)
        out[f"M{l}"] = (y + 8, LANES)
        out[f"N{l}"] = (y, LANES)
    return {k: pltpu.VMEM(v, f32) for k, v in out.items()}


def kernel(dims, counts, names, cells, u, f, out, *scratch):
    b = dict(zip(names, scratch[:-2]))
    send_sem, recv_sem = scratch[-2:]
    here = {a: lax.axis_index(a) for a in AXES}
    serial = itertools.count()

    def device(offset):
        return tuple(lax.rem(here[a] + (o % n), n) for a, o, n in zip(AXES, offset, counts))

    def copy(src, dst, offset):
        k = next(serial)
        c = pltpu.make_async_remote_copy(
            src_ref=src,
            dst_ref=dst,
            send_sem=send_sem.at[k],
            recv_sem=recv_sem.at[k],
            device_id=device(offset),
            device_id_type=pl.DeviceIdType.MESH,
        )
        c.start()
        return c

    def wait(copies):
        for c in copies:
            c.wait()

    offsets = []
    for sign in (1, -1):
        for o in itertools.product((0, 1), repeat=3):
            if any(o):
                offsets.append(tuple(sign * v for v in o))
    for a in range(3):
        for j in range(2, counts[a] - 1):
            offsets.append(tuple(j if i == a else 0 for i in range(3)))
    barrier = pltpu.get_barrier_semaphore()
    for o in offsets:
        pl.semaphore_signal(
            barrier, inc=1, device_id=device(o), device_id_type=pl.DeviceIdType.MESH
        )
    pl.semaphore_wait(barrier, len(offsets))

    def exchange(l, r, v):
        x = dims[l][0]
        hx, hy, hz = (b[f"h{a}{l}"] for a in "xyz")
        yp, zp = b[f"yp{l}"], b[f"zp{l}"]
        return [
            copy(yp.at[1], hy.at[r, 0], (0, 1, 0)),
            copy(yp.at[0], hy.at[r, 1], (0, -1, 0)),
            copy(zp.at[1], hz.at[r, 0], (0, 0, 1)),
            copy(zp.at[0], hz.at[r, 1], (0, 0, -1)),
            copy(v.at[x - 1], hx.at[r, 0], (1, 0, 0)),
            copy(v.at[0], hx.at[r, 1], (-1, 0, 0)),
        ]

    def corner_exchange(kind, l, v):
        x, y, _ = dims[l]
        hi = kind == "r"
        s = 1 if hi else -1
        side = 1 if hi else 0
        yp, zp = b[f"yp{l}"].at[side], b[f"zp{l}"].at[side]
        hx, hy, hz, hw = (b[f"{kind}{a}{l}"] for a in "xyzw")
        ye = yp.at[pl.ds(x - 8 if hi else 0, 8)]
        ze = zp.at[pl.ds(y - 8 if hi else 0, 8)]
        return [
            copy(ze, hw.at[pl.ds(y, 8)], (s, s, s)),
            copy(zp, hw.at[pl.ds(0, y)], (s, 0, s)),
            copy(ze, hz.at[pl.ds(y, 8)], (0, s, s)),
            copy(ye, hy.at[pl.ds(x, 8)], (s, s, 0)),
            copy(yp, hy.at[pl.ds(0, x)], (0, s, 0)),
            copy(zp, hz.at[pl.ds(0, y)], (0, 0, s)),
            copy(v.at[x - 1 if hi else 0], hx, (s, 0, 0)),
        ]

    def zero_acc(l):
        z = jnp.zeros((dims[l][1], LANES), jnp.float32)
        return (z, z)

    def pack(l, x, new, acc):
        _, y, z = dims[l]
        yp = b[f"yp{l}"]
        yp[0, pl.ds(x, 1), :] = new[:1]
        yp[1, pl.ds(x, 1), :] = new[y - 1 :]
        lane = lax.broadcasted_iota(jnp.int32, (y, LANES), 1)
        last = (z - 1) % LANES
        low = pltpu.roll(new[:, :LANES], x, 1)
        high = pltpu.roll(new[:, -LANES:], turn(x + (LANES - last)), 1)
        return (jnp.where(lane == x, low, acc[0]), jnp.where(lane == x, high, acc[1]))

    def store_acc(l, acc):
        b[f"zp{l}"][0] = acc[0]
        b[f"zp{l}"][1] = acc[1]

    def planes(l, body, packed=True):
        def step(i, acc):
            new = body(i)
            return pack(l, i, new, acc) if packed else acc

        acc = lax.fori_loop(0, dims[l][0], step, zero_acc(l))
        if packed:
            store_acc(l, acc)

    def sweep(l, r, src, dst, g, defect=False, shift=None, packed=True):
        x, y, z = dims[l]
        zl = lane_pad(z)
        scale = 0.25**l
        hx, hy, hz = (b[f"h{a}{l}"].at[r] for a in "xyz")
        row, lane = iotas((y, zl))
        last = (z - 1) % LANES

        def plane(i, before, after, acc):
            c = src[i]
            up = jnp.where(row == 0, hy[0, pl.ds(i, 1), :], pltpu.roll(c, 1, 0))
            down = jnp.where(row == y - 1, hy[1, pl.ds(i, 1), :], pltpu.roll(c, y - 1, 0))
            left = pltpu.roll(hz[0], turn(LANES - i), 1)
            left = jnp.where(lane == 0, tile_up(left, zl), pltpu.roll(c, 1, 1))
            right = pltpu.roll(hz[1], turn(LANES + last - i), 1)
            right = jnp.where(lane == z - 1, tile_up(right, zl), pltpu.roll(c, zl - 1, 1))
            beside = (after + before) + (up + down) + (left + right)
            if defect:
                new = g[i] - scale * (6.0 * c - beside)
            else:
                new = (1.0 - relax_weight) * c + (relax_weight / 6.0) * beside
                new = new + (relax_weight / (6.0 * scale)) * g[i]
                if shift is not None:
                    new = new - shift
            dst[i] = new
            return pack(l, i, new, acc) if packed else acc

        def inner(i, acc):
            return plane(i, src[i - 1], src[i + 1], acc)

        acc = plane(0, hx[0], src[1], zero_acc(l))
        acc = lax.fori_loop(1, x - 1, inner, acc)
        acc = plane(x - 1, src[x - 2], hx[1], acc)
        if packed:
            store_acc(l, acc)

    def halves(v):
        return [v[:, k : k + LANES] for k in range(0, v.shape[1], LANES)]

    def restrict_y(ref, row_before):
        n = ref.shape[1] // 2
        parts = []
        first = lax.broadcasted_iota(jnp.int32, (n, LANES), 0) == 0
        for t, rim in enumerate(halves(row_before)):
            even = ref[t, pl.ds(0, n, stride=2), :]
            odd = ref[t, pl.ds(1, n, stride=2), :]
            below = jnp.where(first, rim, pltpu.roll(odd, 1, 0))
            parts.append(0.25 * below + 0.5 * even + 0.25 * odd)
        return jnp.concatenate(parts, 1) if len(parts) > 1 else parts[0]

    def restrict_down(l, d, mean):
        x, y, z = dims[l]
        zl = lane_pad(z)
        xc, yc, zc = dims[l + 1]
        zlc = lane_pad(zc)
        hx, hy, hz, hw = (b[f"r{a}{l}"] for a in "xyzw")
        s, t = b[f"S{l}"], b[f"T{l}"]
        m, n = b[f"M{l}"], b[f"N{l}"]
        lane = lax.broadcasted_iota(jnp.int32, (y + 8, LANES), 1)
        moved = pltpu.roll(hw[...], LANES - x, 1)
        rim = jnp.where(lane == LANES - 1, moved, hz[...])
        m[...] = dot_exact(rim, restrict_matrix(LANES, LANES, xc, LANES - 1))
        n[...] = m[pl.ds(0, y), :]
        even = n[pl.ds(0, yc, stride=2), :]
        odd = n[pl.ds(1, yc, stride=2), :]
        first = lax.broadcasted_iota(jnp.int32, (yc, LANES), 0) == 0
        below = jnp.where(first, m[pl.ds(y + 7, 1), :], pltpu.roll(odd, 1, 0))
        n[pl.ds(0, yc), :] = 0.25 * (0.25 * below + 0.5 * even + 0.25 * odd)

        def plane(i, before, before_row):
            dx = 0.25 * before + 0.5 * d[2 * i] + 0.25 * d[2 * i + 1]
            for k, part in enumerate(halves(dx)):
                s[k] = part
            rows = 0.25 * before_row + 0.5 * hy[pl.ds(2 * i, 1), :]
            rows = rows + 0.25 * hy[pl.ds(2 * i + 1, 1), :]
            t[i] = restrict_y(s, rows)

        def inner(i, _):
            plane(i, d[2 * i - 1], hy[pl.ds(2 * i - 1, 1), :])
            return 0

        plane(0, hx[...], hy[pl.ds(x + 7, 1), :])
        lax.fori_loop(1, xc, inner, 0)
        g, v = b[f"G{l + 1}"], b[f"A{l + 1}"]
        w = restrict_matrix(zl, zlc, zc)
        chunk = 8

        def multiply(k, _):
            rows = t[pl.ds(k * chunk, chunk)].reshape(chunk * yc, zl)
            g[pl.ds(k * chunk, chunk)] = dot_exact(rows, w).reshape(chunk, yc, zlc)
            return 0

        lax.fori_loop(0, xc // chunk, multiply, 0)
        lane_c = lax.broadcasted_iota(jnp.int32, (yc, zlc), 1)

        def finish(i):
            col = pltpu.roll(n[pl.ds(0, yc), :], turn(LANES - i), 1)
            new = g[i] + jnp.where(lane_c == 0, tile_up(col, zlc), 0.0)
            if mean is not None:
                new = new - mean
            g[i] = new
            new = (relax_weight / (6.0 * 0.25 ** (l + 1))) * new
            v[i] = new
            return new

        planes(l + 1, finish)

    def prolong_up(l, c, v, work, shift):
        x, y, z = dims[l]
        zl = lane_pad(z)
        xc, yc, zc = dims[l + 1]
        zlc = lane_pad(zc)
        hx, hy, hz, hw = (b[f"p{a}{l + 1}"] for a in "xyzw")
        s, t, th, ty = b[f"S{l}"], b[f"T{l}"], b[f"TH{l}"], b[f"TY{l}"]
        m = b[f"M{l + 1}"]
        lane = lax.broadcasted_iota(jnp.int32, (yc + 8, LANES), 1)
        m[...] = 0.5 * jnp.where(lane == xc, pltpu.roll(hw[...], xc, 1), hz[...])
        w = prolong_matrix(zlc, zl, zc)
        chunk = 8

        def multiply(k, _):
            rows = c[pl.ds(k * chunk, chunk)].reshape(chunk * yc, zlc)
            t[pl.ds(k * chunk, chunk)] = dot_exact(rows, w).reshape(chunk, yc, zl)
            return 0

        lax.fori_loop(0, xc // chunk, multiply, 0)
        th[...] = dot_exact(hx[...], w)
        ty[...] = dot_exact(hy[...], w)
        at_end = lane == LANES - 1
        final = lax.broadcasted_iota(jnp.int32, (yc, LANES), 0) == yc - 1

        def plane(i, values):
            add = pltpu.roll(m[...], turn(2 * LANES - 1 - i), 1)
            add = jnp.where(at_end, add, 0.0)
            rim = ty[pl.ds(i, 1), :]
            rims, parts = halves(rim), halves(values)
            parts[-1] = parts[-1] + add[:yc]
            rims[-1] = rims[-1] + add[yc : yc + 1]
            for k, (part, edge) in enumerate(zip(parts, rims)):
                above = jnp.where(final, edge, pltpu.roll(part, yc - 1, 0))
                s[k, pl.ds(0, yc, stride=2), :] = part
                s[k, pl.ds(1, yc, stride=2), :] = 0.5 * (part + above)
            full = [s[k] for k in range(len(parts))]
            work[i] = jnp.concatenate(full, 1) if len(full) > 1 else full[0]

        def spread(i, _):
            plane(i, t[i])
            return 0

        lax.fori_loop(0, xc, spread, 0)
        plane(xc, th[...])

        def add(i, acc):
            low, high = work[i], work[i + 1]
            if shift is not None:
                low, high = low - shift, high - shift
            even = v[2 * i] + low
            odd = v[2 * i + 1] + 0.5 * (low + high)
            v[2 * i] = even
            v[2 * i + 1] = odd
            return pack(l, 2 * i + 1, odd, pack(l, 2 * i, even, acc))

        store_acc(l, lax.fori_loop(0, xc, add, zero_acc(l)))

    st, sg = b["stats"], [b[f"sums{a}"] for a in range(3)]

    def spread_sums(a):
        return [
            copy(st.at[a], sg[a].at[j], tuple(j if i == a else 0 for i in range(3)))
            for j in range(1, counts[a])
        ]

    def gather_sums(a, copies):
        wait(copies)
        total = st[a]
        for j in range(1, counts[a]):
            total = total + sg[a][j]
        if a < 2:
            st[a + 1] = total
        return total

    x0, y0, z0 = dims[0]

    def folded(v):
        return jnp.sum(v.reshape(y0 // 8, 8, z0), 0)

    def first(i, carry):
        total, acc = carry
        v = u[i]
        return total + folded(v), pack(0, i, v, acc)

    none = jnp.zeros((8, z0), jnp.float32)
    total_u, acc = lax.fori_loop(0, x0, first, (none, zero_acc(0)))
    store_acc(0, acc)
    moving = exchange(0, 0, u)
    total_f = lax.fori_loop(0, x0, lambda i, t: t + folded(f[i]), none)
    st[0, 0] = total_u
    st[0, 1] = total_f
    sums = spread_sums(0)
    a0, b0, a1, b1 = b["A0"], b["B0"], b["A1"], b["B1"]
    a2, b2 = b["A2"], b["B2"]
    wait(moving)
    sweep(0, 0, u, a0, f)
    moving = exchange(0, 1, a0)
    gather_sums(0, sums)
    sums = spread_sums(1)
    wait(moving)
    sweep(0, 1, a0, b0, f)
    moving = exchange(0, 2, b0)
    gather_sums(1, sums)
    sums = spread_sums(2)
    wait(moving)
    sweep(0, 2, b0, a0, f, defect=True)
    moving = corner_exchange("r", 0, a0)
    total = gather_sums(2, sums)
    mean_u = jnp.sum(total[0]) * (1.0 / cells)
    mean_f = jnp.sum(total[1]) * (1.0 / cells)
    gain = relax_weight / 6.0
    wait(moving)
    restrict_down(0, a0, mean_f)

    wait(exchange(1, 0, a1))
    sweep(1, 0, a1, b1, b["G1"])
    wait(exchange(1, 1, b1))
    sweep(1, 1, b1, a1, b["G1"], defect=True)
    wait(corner_exchange("r", 1, a1))
    restrict_down(1, a1, None)

    v, w = a2, b2
    for k in range(COARSE_SWEEPS - 1):
        wait(exchange(2, k, v))
        sweep(2, k, v, w, b["G2"])
        v, w = w, v
    wait(corner_exchange("p", 2, v))
    prolong_up(1, v, b1, a1, None)
    wait(exchange(1, 2, b1))
    sweep(1, 2, b1, a1, b["G1"])
    wait(exchange(1, 3, a1))
    sweep(1, 3, a1, b1, b["G1"])
    wait(corner_exchange("p", 1, b1))
    prolong_up(0, b1, b0, a0, mean_u + 2.0 * gain * mean_f)
    wait(exchange(0, 3, b0))
    sweep(0, 3, b0, a0, f, shift=gain * mean_f)
    wait(exchange(0, 4, a0))
    sweep(0, 4, a0, out, f, shift=gain * mean_f, packed=False)


def solution(mesh):
    counts = tuple(mesh.shape[a] for a in AXES)

    def shards(right_side, initial_guess):
        shape = right_side.shape
        dims = tuple(tuple(n >> l for n in shape) for l in range(3))
        cells = float(right_side.size)
        for n in counts:
            cells *= n
        bufs = buffers(dims)
        bufs["stats"] = pltpu.VMEM((3, 2, 8, shape[2]), jnp.float32)
        for a in range(3):
            bufs[f"sums{a}"] = pltpu.VMEM((counts[a], 2, 8, shape[2]), jnp.float32)
        messages = 6 * (9 + COARSE_SWEEPS - 1) + 7 * 4 + sum(counts) - 3
        vmem = pl.BlockSpec(memory_space=pltpu.VMEM)
        return pl.pallas_call(
            functools.partial(kernel, dims, counts, tuple(bufs), cells),
            out_shape=jax.ShapeDtypeStruct(shape, jnp.float32),
            in_specs=[vmem, vmem],
            out_specs=vmem,
            scratch_shapes=list(bufs.values())
            + [pltpu.SemaphoreType.DMA((messages,)), pltpu.SemaphoreType.DMA((messages,))],
            compiler_params=pltpu.CompilerParams(
                collective_id=0, has_side_effects=True, vmem_limit_bytes=48 * 1024 * 1024
            ),
        )(initial_guess, right_side)

    placed = (P(*AXES), P(*AXES))
    return jax.shard_map(
        shards, mesh=mesh, in_specs=placed, out_specs=P(*AXES), check_vma=False
    )
```

time: 596 us -> 205 us (0.34); the launches traced: 587 us -> 205 us
  Pallas kernels: 0 us -> 203 us
  local copies, waits for them, and re-layouts: 168 us -> 2.02 us
  other arithmetic: 160 us -> 0 us
  waiting for transfers between devices: 100 us -> 0 us
  starting transfers between devices: 97.3 us -> 0 us
  blocking collectives: 58.8 us -> 0 us
    pallas_call x0 -> x1, Pallas kernels: none -> 203 us  [shards(): pl.pallas_call(functools.partial(kernel, dims, counts, tuple(bufs), cells...]
    slice x76 -> x0, local copies, waits for them, and re-layouts: 116 us -> none  [the longest x20 28.5 us: padded_2(): lax.slice_in_dim(block, 0, width, axis=dim)]
    add x20 -> x0, other arithmetic: 106 us -> none  [the longest x12 97.4 us: relax_step(): centre + relax_weight * (source / (6.0 * level_scale) - centre + beside /...]
    ppermute x76 -> x0, waiting for transfers between devices: 100 us -> none  [the longest x32 58.3 us: padded_2(): lax.ppermute(lax.slice_in_dim(block, block.shape[dim] - width, None, axis...]
    ppermute x76 -> x0, starting transfers between devices: 97.3 us -> none  [the longest x32 46.2 us: padded_2(): lax.ppermute(lax.slice_in_dim(block, 0, width, axis=dim), axis, backward)]
    psum x1 -> x0, blocking collectives: 42.2 us -> none  [shards(): lax.psum((jnp.sum(right_side), jnp.sum(initial_guess)), ('gx', 'gy', 'gz'))]
    sub x3 -> x0, other arithmetic: 26.3 us -> none  [the longest x2 23.8 us: defect_of(): return source - level_scale * (6.0 * centre - beside)]
    ppermute x21 -> x0, local copies, waits for them, and re-layouts: 21.1 us -> none  [the longest x10 14.1 us: padded_2(): lax.ppermute(lax.slice_in_dim(block, block.shape[dim] - width, None, axis...]
  transfers between devices with their start and end apart: 76 -> 0, of which waited for: 56 -> 0; matrix products, arithmetic and copies ran while one was open for 19% -> 0% of each run, Pallas kernels for 0% -> 0%
where the time goes in v1:
time: 205 us
  Pallas kernels  203 us (99%)
    pallas_call x1, Pallas kernels, shards(): pl.pallas_call(functools.partial(kernel, dims, counts, tuple(bufs), cells...  203 us

profile of v1, /device:TPU:0, one launch (start us, length us, event | category | flops | bytes accessed | tf_op | source)
XLA Modules:
  0.0 204.9 jit_solution(10026895427451316030)
XLA Ops:
  0.0 202.8 %shard_map.28 = f32[64,64,256]{2,1,0:T(8,128)S(1)} custom-call(f32[64,64,256]{2,1,0:T(8,128)} %u.1, f32[64,64,256]{2,1,0:T(8,128)} %f.1), custom_call_target="tpu_custom_call" | custom-call | tf_op jit(solution)/shard_map/pallas_call | solution.py:454
  202.9 2.0 copy.4

commit v2 on v1

--- a/solution.py
+++ b/solution.py
@@ -133,14 +133,22 @@
         x = dims[l][0]
         hx, hy, hz = (b[f"h{a}{l}"] for a in "xyz")
         yp, zp = b[f"yp{l}"], b[f"zp{l}"]
-        return [
-            copy(yp.at[1], hy.at[r, 0], (0, 1, 0)),
-            copy(yp.at[0], hy.at[r, 1], (0, -1, 0)),
-            copy(zp.at[1], hz.at[r, 0], (0, 0, 1)),
-            copy(zp.at[0], hz.at[r, 1], (0, 0, -1)),
-            copy(v.at[x - 1], hx.at[r, 0], (1, 0, 0)),
-            copy(v.at[0], hx.at[r, 1], (-1, 0, 0)),
-        ]
+
+        def early():
+            return [
+                copy(v.at[x - 1], hx.at[r, 0], (1, 0, 0)),
+                copy(v.at[0], hx.at[r, 1], (-1, 0, 0)),
+            ]
+
+        def late():
+            return [
+                copy(yp.at[1], hy.at[r, 0], (0, 1, 0)),
+                copy(yp.at[0], hy.at[r, 1], (0, -1, 0)),
+                copy(zp.at[1], hz.at[r, 0], (0, 0, 1)),
+                copy(zp.at[0], hz.at[r, 1], (0, 0, -1)),
+            ]
+
+        return early, late
 
     def corner_exchange(kind, l, v):
         x, y, _ = dims[l]
@@ -151,15 +159,24 @@
         hx, hy, hz, hw = (b[f"{kind}{a}{l}"] for a in "xyzw")
         ye = yp.at[pl.ds(x - 8 if hi else 0, 8)]
         ze = zp.at[pl.ds(y - 8 if hi else 0, 8)]
-        return [
-            copy(ze, hw.at[pl.ds(y, 8)], (s, s, s)),
-            copy(zp, hw.at[pl.ds(0, y)], (s, 0, s)),
-            copy(ze, hz.at[pl.ds(y, 8)], (0, s, s)),
-            copy(ye, hy.at[pl.ds(x, 8)], (s, s, 0)),
-            copy(yp, hy.at[pl.ds(0, x)], (0, s, 0)),
-            copy(zp, hz.at[pl.ds(0, y)], (0, 0, s)),
-            copy(v.at[x - 1 if hi else 0], hx, (s, 0, 0)),
-        ]
+
+        def early():
+            return [copy(v.at[x - 1 if hi else 0], hx, (s, 0, 0))]
+
+        def late():
+            return [
+                copy(ze, hw.at[pl.ds(y, 8)], (s, s, s)),
+                copy(zp, hw.at[pl.ds(0, y)], (s, 0, s)),
+                copy(ze, hz.at[pl.ds(y, 8)], (0, s, s)),
+                copy(ye, hy.at[pl.ds(x, 8)], (s, s, 0)),
+                copy(yp, hy.at[pl.ds(0, x)], (0, s, 0)),
+                copy(zp, hz.at[pl.ds(0, y)], (0, 0, s)),
+            ]
+
+        return early, late
+
+    def both(parts):
+        return parts[0]() + parts[1]()
 
     def zero_acc(l):
         z = jnp.zeros((dims[l][1], LANES), jnp.float32)
@@ -189,23 +206,22 @@
         if packed:
             store_acc(l, acc)
 
-    def sweep(l, r, src, dst, g, defect=False, shift=None, packed=True):
+    def sweep(l, r, moving, src, dst, g, onward=None, defect=False, shift=None):
         x, y, z = dims[l]
         zl = lane_pad(z)
         scale = 0.25**l
         hx, hy, hz = (b[f"h{a}{l}"].at[r] for a in "xyz")
         row, lane = iotas((y, zl))
         last = (z - 1) % LANES
-
-        def plane(i, before, after, acc):
+        gain = scale if defect else relax_weight / 6.0
+
+        def plane(i, around):
             c = src[i]
-            up = jnp.where(row == 0, hy[0, pl.ds(i, 1), :], pltpu.roll(c, 1, 0))
-            down = jnp.where(row == y - 1, hy[1, pl.ds(i, 1), :], pltpu.roll(c, y - 1, 0))
-            left = pltpu.roll(hz[0], turn(LANES - i), 1)
-            left = jnp.where(lane == 0, tile_up(left, zl), pltpu.roll(c, 1, 1))
-            right = pltpu.roll(hz[1], turn(LANES + last - i), 1)
-            right = jnp.where(lane == z - 1, tile_up(right, zl), pltpu.roll(c, zl - 1, 1))
-            beside = (after + before) + (up + down) + (left + right)
+            up = jnp.where(row == 0, 0.0, pltpu.roll(c, 1, 0))
+            down = jnp.where(row == y - 1, 0.0, pltpu.roll(c, y - 1, 0))
+            left = jnp.where(lane == 0, 0.0, pltpu.roll(c, 1, 1))
+            right = jnp.where(lane == z - 1, 0.0, pltpu.roll(c, zl - 1, 1))
+            beside = around + (up + down) + (left + right)
             if defect:
                 new = g[i] - scale * (6.0 * c - beside)
             else:
@@ -214,16 +230,43 @@
                 if shift is not None:
                     new = new - shift
             dst[i] = new
-            return pack(l, i, new, acc) if packed else acc
-
-        def inner(i, acc):
-            return plane(i, src[i - 1], src[i + 1], acc)
-
-        acc = plane(0, hx[0], src[1], zero_acc(l))
-        acc = lax.fori_loop(1, x - 1, inner, acc)
-        acc = plane(x - 1, src[x - 2], hx[1], acc)
-        if packed:
+
+        def inner(i, _):
+            plane(i, src[i - 1] + src[i + 1])
+            return 0
+
+        plane(0, src[1])
+        lax.fori_loop(1, x - 1, inner, 0)
+        plane(x - 1, src[x - 2])
+        wait(moving)
+        row8 = lax.broadcasted_iota(jnp.int32, (8, zl), 0)
+        lane1 = lax.broadcasted_iota(jnp.int32, (y, LANES), 1)
+
+        def fix(i, acc, beyond=None):
+            new = dst[i]
+            if beyond is not None:
+                new = new + gain * beyond
+            top = new[:8] + jnp.where(row8 == 0, gain * hy[0, pl.ds(i, 1), :], 0.0)
+            new = jnp.concatenate([top, new[8:]], 0) if y > 8 else top
+            end = new[y - 8 :] + jnp.where(row8 == 7, gain * hy[1, pl.ds(i, 1), :], 0.0)
+            new = jnp.concatenate([new[: y - 8], end], 0) if y > 8 else end
+            parts = halves(new)
+            left = pltpu.roll(hz[0], turn(LANES - i), 1)
+            right = pltpu.roll(hz[1], turn(LANES + last - i), 1)
+            parts[0] = parts[0] + jnp.where(lane1 == 0, gain * left, 0.0)
+            parts[-1] = parts[-1] + jnp.where(lane1 == last, gain * right, 0.0)
+            new = jnp.concatenate(parts, 1) if len(parts) > 1 else parts[0]
+            dst[i] = new
+            return pack(l, i, new, acc) if onward is not None else acc
+
+        acc = fix(0, zero_acc(l), hx[0])
+        acc = fix(x - 1, acc, hx[1])
+        started = onward[0]() if onward is not None else []
+        acc = lax.fori_loop(1, x - 1, fix, acc)
+        if onward is not None:
             store_acc(l, acc)
+            started = started + onward[1]()
+        return started
 
     def halves(v):
         return [v[:, k : k + LANES] for k in range(0, v.shape[1], LANES)]
@@ -383,26 +426,21 @@
     none = jnp.zeros((8, z0), jnp.float32)
     total_u, acc = lax.fori_loop(0, x0, first, (none, zero_acc(0)))
     store_acc(0, acc)
-    moving = exchange(0, 0, u)
+    moving = both(exchange(0, 0, u))
     total_f = lax.fori_loop(0, x0, lambda i, t: t + folded(f[i]), none)
     st[0, 0] = total_u
     st[0, 1] = total_f
     sums = spread_sums(0)
     a0, b0, a1, b1 = b["A0"], b["B0"], b["A1"], b["B1"]
     a2, b2 = b["A2"], b["B2"]
-    wait(moving)
-    sweep(0, 0, u, a0, f)
-    moving = exchange(0, 1, a0)
+    g1, g2 = b["G1"], b["G2"]
+    moving = sweep(0, 0, moving, u, a0, f, exchange(0, 1, a0))
     gather_sums(0, sums)
     sums = spread_sums(1)
-    wait(moving)
-    sweep(0, 1, a0, b0, f)
-    moving = exchange(0, 2, b0)
+    moving = sweep(0, 1, moving, a0, b0, f, exchange(0, 2, b0))
     gather_sums(1, sums)
     sums = spread_sums(2)
-    wait(moving)
-    sweep(0, 2, b0, a0, f, defect=True)
-    moving = corner_exchange("r", 0, a0)
+    moving = sweep(0, 2, moving, b0, a0, f, corner_exchange("r", 0, a0), defect=True)
     total = gather_sums(2, sums)
     mean_u = jnp.sum(total[0]) * (1.0 / cells)
     mean_f = jnp.sum(total[1]) * (1.0 / cells)
@@ -410,30 +448,29 @@
     wait(moving)
     restrict_down(0, a0, mean_f)
 
-    wait(exchange(1, 0, a1))
-    sweep(1, 0, a1, b1, b["G1"])
-    wait(exchange(1, 1, b1))
-    sweep(1, 1, b1, a1, b["G1"], defect=True)
-    wait(corner_exchange("r", 1, a1))
+    moving = both(exchange(1, 0, a1))
+    moving = sweep(1, 0, moving, a1, b1, g1, exchange(1, 1, b1))
+    moving = sweep(1, 1, moving, b1, a1, g1, corner_exchange("r", 1, a1), defect=True)
+    wait(moving)
     restrict_down(1, a1, None)
 
     v, w = a2, b2
+    moving = both(exchange(2, 0, v))
     for k in range(COARSE_SWEEPS - 1):
-        wait(exchange(2, k, v))
-        sweep(2, k, v, w, b["G2"])
+        final = k == COARSE_SWEEPS - 2
+        onward = corner_exchange("p", 2, w) if final else exchange(2, k + 1, w)
+        moving = sweep(2, k, moving, v, w, g2, onward)
         v, w = w, v
-    wait(corner_exchange("p", 2, v))
+    wait(moving)
     prolong_up(1, v, b1, a1, None)
-    wait(exchange(1, 2, b1))
-    sweep(1, 2, b1, a1, b["G1"])
-    wait(exchange(1, 3, a1))
-    sweep(1, 3, a1, b1, b["G1"])
-    wait(corner_exchange("p", 1, b1))
+    moving = both(exchange(1, 2, b1))
+    moving = sweep(1, 2, moving, b1, a1, g1, exchange(1, 3, a1))
+    moving = sweep(1, 3, moving, a1, b1, g1, corner_exchange("p", 1, b1))
+    wait(moving)
     prolong_up(0, b1, b0, a0, mean_u + 2.0 * gain * mean_f)
-    wait(exchange(0, 3, b0))
-    sweep(0, 3, b0, a0, f, shift=gain * mean_f)
-    wait(exchange(0, 4, a0))
-    sweep(0, 4, a0, out, f, shift=gain * mean_f, packed=False)
+    moving = both(exchange(0, 3, b0))
+    moving = sweep(0, 3, moving, b0, a0, f, exchange(0, 4, a0), shift=gain * mean_f)
+    sweep(0, 4, moving, a0, out, f, shift=gain * mean_f)
 
 
 def solution(mesh):

time: 205 us -> 199 us (0.971)
  Pallas kernels: 203 us -> 197 us
    pallas_call x1, Pallas kernels: 203 us -> 197 us  [shards(): pl.pallas_call(functools.partial(kernel, dims, counts, tuple(bufs), cells...]
where the time goes in v2:
time: 199 us
  Pallas kernels  197 us (99%)
  local copies, waits for them, and re-layouts  2.02 us (1%)
    pallas_call x1, Pallas kernels, shards(): pl.pallas_call(functools.partial(kernel, dims, counts, tuple(bufs), cells...  197 us

profile of v2, /device:TPU:0, one launch (start us, length us, event | category | flops | bytes accessed | tf_op | source)
XLA Modules:
  0.0 199.2 jit_solution(4037678567749165378)
XLA Ops:
  0.0 197.2 %shard_map.28 = f32[64,64,256]{2,1,0:T(8,128)S(1)} custom-call(f32[64,64,256]{2,1,0:T(8,128)} %u.1, f32[64,64,256]{2,1,0:T(8,128)} %f.1), custom_call_target="tpu_custom_call" | custom-call | tf_op jit(solution)/shard_map/pallas_call | solution.py:491
  197.2 2.0 %copy.4 = f32[64,64,256]{2,1,0:T(8,128)} copy(f32[64,64,256]{2,1,0:T(8,128)S(1)} %shard_map.28) | data formatting | bytes 8388608

commit v3 on v2

--- a/solution.py
+++ b/solution.py
@@ -88,9 +88,14 @@
     return {k: pltpu.VMEM(v, f32) for k, v in out.items()}
 
 
-def kernel(dims, counts, names, cells, u, f, out, *scratch):
-    b = dict(zip(names, scratch[:-2]))
-    send_sem, recv_sem = scratch[-2:]
+def kernel(dims, counts, names, cells, u_far, f_far, out, *scratch):
+    b = dict(zip(names, scratch[:-3]))
+    send_sem, recv_sem, load_sem = scratch[-3:]
+    u, f = b["u"], b["f"]
+    load_u = pltpu.make_async_copy(u_far, u, load_sem.at[0])
+    load_f = pltpu.make_async_copy(f_far, f, load_sem.at[1])
+    load_u.start()
+    load_f.start()
     here = {a: lax.axis_index(a) for a in AXES}
     serial = itertools.count()
 
@@ -424,9 +429,11 @@
         return total + folded(v), pack(0, i, v, acc)
 
     none = jnp.zeros((8, z0), jnp.float32)
+    load_u.wait()
     total_u, acc = lax.fori_loop(0, x0, first, (none, zero_acc(0)))
     store_acc(0, acc)
     moving = both(exchange(0, 0, u))
+    load_f.wait()
     total_f = lax.fori_loop(0, x0, lambda i, t: t + folded(f[i]), none)
     st[0, 0] = total_u
     st[0, 1] = total_f
@@ -483,6 +490,8 @@
         for n in counts:
             cells *= n
         bufs = buffers(dims)
+        bufs["u"] = pltpu.VMEM(shape, jnp.float32)
+        bufs["f"] = pltpu.VMEM(shape, jnp.float32)
         bufs["stats"] = pltpu.VMEM((3, 2, 8, shape[2]), jnp.float32)
         for a in range(3):
             bufs[f"sums{a}"] = pltpu.VMEM((counts[a], 2, 8, shape[2]), jnp.float32)
@@ -491,10 +500,10 @@
         return pl.pallas_call(
             functools.partial(kernel, dims, counts, tuple(bufs), cells),
             out_shape=jax.ShapeDtypeStruct(shape, jnp.float32),
-            in_specs=[vmem, vmem],
+            in_specs=[pl.BlockSpec(memory_space=pl.ANY)] * 2,
             out_specs=vmem,
             scratch_shapes=list(bufs.values())
-            + [pltpu.SemaphoreType.DMA((messages,)), pltpu.SemaphoreType.DMA((messages,))],
+            + [pltpu.SemaphoreType.DMA((n,)) for n in (messages, messages, 2)],
             compiler_params=pltpu.CompilerParams(
                 collective_id=0, has_side_effects=True, vmem_limit_bytes=48 * 1024 * 1024
             ),

time: 199 us -> 196 us (0.985)
  Pallas kernels: 197 us -> 193 us
    pallas_call x1, Pallas kernels: 197 us -> 193 us  [shards(): pl.pallas_call(functools.partial(kernel, dims, counts, tuple(bufs), cells...]
where the time goes in v3:
time: 196 us; the launch traced here: 195 us
  Pallas kernels  193 us (98%)
  local copies, waits for them, and re-layouts  2.02 us (1%)
    pallas_call x1, Pallas kernels, shards(): pl.pallas_call(functools.partial(kernel, dims, counts, tuple(bufs), cells...  193 us

profile of v3, /device:TPU:0, one launch (start us, length us, event | category | flops | bytes accessed | tf_op | source)
XLA Modules:
  0.0 195.4 jit_solution(15568199373817410917)
XLA Ops:
  0.0 193.4 %shard_map.28 = f32[64,64,256]{2,1,0:T(8,128)S(1)} custom-call(f32[64,64,256]{2,1,0:T(8,128)} %u_far.1, f32[64,64,256]{2,1,0:T(8,128)} %f_far.1), custom_call_target="tpu_custom_call" | custom-call | tf_op jit(solution)/shard_map/pallas_call | solution.py:500
  193.4 2.0 %copy.4 = f32[64,64,256]{2,1,0:T(8,128)} copy(f32[64,64,256]{2,1,0:T(8,128)S(1)} %shard_map.28) | data formatting | bytes 8388608
